TPU v7x, 32 devices: a whole 2x2x4 slice. The times are simulated.
32 devices in a mesh: lat: 8 (over z, y), ch: 4 (over x, core).
Axes of the slice: x: 2, y: 2, z: 4, core: 2. Of those that a mesh axis runs over, the one named last changes fastest.
Arguments:
- field: bfloat16 [728, 256, 1440], P('lat', 'ch'), may hold values from -6 to 6
- legendre: bfloat16 [384, 721, 728], P(('lat', 'ch')), may hold values from -0.21875 to 0.21875
- pair_order: int32 [384], replicated, may hold values from 0 to 383, each once
Outputs:
- coeffs: float32 [384, 721, 2, 256], P(('lat', 'ch'))
Inputs may be any that keep to these rules, and one draw needn't show every extreme that they name: `pair_order`: each of 0 to 383 appears once; a value p below 360 gives its bin the orders p and 719 - p, and a bin with a larger value is empty.
All inputs are finite; a program needn't handle non-finite values.
Results may differ from a plain program's by a relative error of at most 0.0037.
Values may be sent and summed in bfloat16 or wider, within the bound.
A program may use at most 256 MiB of HBM per device.

v0:
```python
import math

import jax
import jax.numpy as jnp
from jax import lax
from jax.sharding import PartitionSpec as P

NLAT = 721
GROUPS = 4


def dft_table(points, modes, lon_count):
    columns = jnp.repeat(modes, 2)
    phase = jnp.tile(jnp.array([0, lon_count // 4], jnp.int32), modes.shape[0])
    turns = (points[:, None] * columns[None, :] + phase[None, :]) % lon_count
    angle = turns.astype(jnp.float32) * (2.0 * math.pi / lon_count)
    return jnp.cos(angle).astype(jnp.bfloat16)


def per_device(field, legendre, pair_order):
    lat_rows, chan_dev, lon_count = field.shape
    own, row_count, _ = legendre.shape
    lat_count = lax.axis_size("lat")
    ch_count = lax.axis_size("ch")
    dev_count = lat_count * ch_count
    me = lax.axis_index("lat") * ch_count + lax.axis_index("ch")
    max_order = row_count - 1
    keep_all = pair_order < max_order // 2
    first_order = jnp.where(keep_all, pair_order, 0)
    orders = jnp.stack([first_order, max_order - 1 - first_order], axis=1)
    bound_own = lax.dynamic_slice_in_dim(max_order - first_order, me * own, own)
    keep_own = lax.dynamic_slice_in_dim(keep_all, me * own, own)
    rows_global = lax.axis_index("lat") * lat_rows + jnp.arange(lat_rows, dtype=jnp.int32)
    in_grid = (rows_global < NLAT)[:, None, None]
    norm_scale = 2.0 * math.pi / lon_count
    points = jnp.arange(lon_count, dtype=jnp.int32)
    degree = jnp.arange(row_count, dtype=jnp.int32)
    groups = math.gcd(GROUPS, own)
    width = own // groups
    by_dev = orders.reshape(dev_count, own, 2)
    outs = []
    for g in range(groups):
        part = by_dev[:, g * width : (g + 1) * width].reshape(-1)
        basis = dft_table(points, part, lon_count)
        fourier = jnp.einsum("ack,kn->anc", field, basis, preferred_element_type=jnp.float32)
        fourier = jnp.where(in_grid, fourier * norm_scale, 0.0).astype(jnp.bfloat16)
        fourier = fourier.reshape(lat_rows, dev_count * width, 4 * chan_dev)
        got = lax.all_to_all(fourier, ("lat", "ch"), split_axis=1, concat_axis=0, tiled=True)
        got = got.reshape(lat_count, ch_count, lat_rows, width, 4, chan_dev)
        got = got.transpose(3, 0, 2, 4, 1, 5)
        got = got.reshape(width, lat_count * lat_rows, 4 * ch_count * chan_dev)
        products = jnp.einsum(
            "brl,bln->brn", legendre[g * width : (g + 1) * width], got, preferred_element_type=jnp.float32
        )
        bound = bound_own[g * width : (g + 1) * width]
        keep = keep_own[g * width : (g + 1) * width]
        upper = degree[None, :, None] < bound[:, None, None]
        half = products.shape[2] // 2
        chosen = jnp.where(upper, products[:, :, :half], products[:, :, half:])
        chosen = chosen * keep[:, None, None].astype(jnp.float32)
        outs.append(chosen.reshape(width, row_count, 2, half // 2))
    return outs[0] if groups == 1 else jnp.concatenate(outs, axis=0)


def solution(mesh):
    in_specs = (P("lat", "ch", None), P(("lat", "ch"), None, None), P())
    out_specs = P(("lat", "ch"), None, None, None)
    return jax.shard_map(
        per_device, mesh=mesh, in_specs=in_specs, out_specs=out_specs, check_vma=False
    )
```

profile of v0, /device:TPU:0, one launch (start us, length us, event | category | flops | bytes accessed | tf_op | source)
XLA Modules:
  0.0 631.1 jit_solution(3836355545497258501)
XLA Ops:
  0.0 0.7 broadcast_subtract_fusion.1
  1.2 0.1 reshape.192
  1.5 0.1 mul.134
  1.8 41.2 %fusion.8 = bf16[91,384,64]{1,0,2:T(8,128)(2,1)} fusion(pred[91]{0:T(512)(128)(4,1)S(1)} %add_compare_fusion, bf16[91,64,1440]{2,1,0:T(8,128)(2,1)} %param.7, s32[384]{0:T(512)S(1)} %add.79, s32[384]{0:T(512)S(1)} %mul.134), kind=kOutput, calls=%fused_computation.13 | convolution fusion | flops 6453669888 | bytes 21249116 | tf_op jit(solution)/shard_map/ack,kn->anc/dot_general | solution.py:45
  42.9 8.6 %copy.44 = bf16[91,384,64]{0,2,1:T(8,128)(2,1)} copy(bf16[91,384,64]{1,0,2:T(8,128)(2,1)} %fusion.8) | data formatting | bytes 8945664 | tf_op jit(solution)/shard_map/convert_element_type | solution.py:46
  51.5 8.3 %copy.45 = bf16[91,96,256]{2,0,1:T(8,128)(2,1)} copy(bf16[91,96,256]{0,2,1:T(8,128)(2,1)} %bitcast.80) | data formatting | bytes 8945664 | tf_op jit(solution)/shard_map/reshape | solution.py:47
  59.8 7.7 %all-to-all-start = ((bf16[91,96,256]{2,0,1:T(8,128)(2,1)}), bf16[91,96,256]{2,0,1:T(8,128)(2,1)}, u32[]{:S(2)}, u32[]{:S(2)}) async-start(bf16[91,96,256]{2,0,1:T(8,128)(2,1)} %copy.45), calls=%async_computation | async-start | bytes 9437184 | tf_op jit(solution)/shard_map/all_to_all | solution.py:48
  67.7 0.1 reshape.197
  68.1 41.2 %fusion.9 = bf16[91,384,64]{1,0,2:T(8,128)(2,1)} fusion(pred[91]{0:T(512)(128)(4,1)S(1)} %add_compare_fusion, bf16[91,64,1440]{2,1,0:T(8,128)(2,1)} %param.7, s32[384]{0:T(512)S(1)} %mul.142, s32[384]{0:T(512)S(1)} %add.79), kind=kOutput, calls=%fused_computation.14 | convolution fusion | flops 6453669888 | bytes 21249116 | tf_op jit(solution)/shard_map/ack,kn->anc/dot_general | solution.py:45
  109.3 8.6 %copy.51 = bf16[91,384,64]{0,2,1:T(8,128)(2,1)} copy(bf16[91,384,64]{1,0,2:T(8,128)(2,1)} %fusion.9) | data formatting | bytes 8945664 | tf_op jit(solution)/shard_map/convert_element_type | solution.py:46
  117.9 8.3 %copy.52 = bf16[91,96,256]{2,0,1:T(8,128)(2,1)} copy(bf16[91,96,256]{0,2,1:T(8,128)(2,1)} %bitcast.81) | data formatting | bytes 8945664 | tf_op jit(solution)/shard_map/reshape | solution.py:47
  126.2 46.4 %all-to-all-done = bf16[91,96,256]{2,0,1:T(8,128)(2,1)} async-done(((bf16[91,96,256]{2,0,1:T(8,128)(2,1)}), bf16[91,96,256]{2,0,1:T(8,128)(2,1)}, u32[]{:S(2)}, u32[]{:S(2)}) %all-to-all-start) | async-done | bytes 4472864 | tf_op jit(solution)/shard_map/all_to_all | solution.py:48
  172.6 4.6 all-to-all-start.1
  177.3 0.1 reshape.202
  177.7 41.3 %fusion.10 = bf16[91,384,64]{1,0,2:T(8,128)(2,1)} fusion(pred[91]{0:T(512)(128)(4,1)S(1)} %add_compare_fusion, bf16[91,64,1440]{2,1,0:T(8,128)(2,1)} %param.7, s32[384]{0:T(512)S(1)} %mul.150, s32[384]{0:T(512)S(1)} %add.79), kind=kOutput, calls=%fused_computation.15 | convolution fusion | flops 6453669888 | bytes 21249116 | tf_op jit(solution)/shard_map/ack,kn->anc/dot_general | solution.py:45
  219.0 8.6 %copy.58 = bf16[91,384,64]{0,2,1:T(8,128)(2,1)} copy(bf16[91,384,64]{1,0,2:T(8,128)(2,1)} %fusion.10) | data formatting | bytes 8945664 | tf_op jit(solution)/shard_map/convert_element_type | solution.py:46
  227.6 8.3 %copy.59 = bf16[91,96,256]{2,0,1:T(8,128)(2,1)} copy(bf16[91,96,256]{0,2,1:T(8,128)(2,1)} %bitcast.82) | data formatting | bytes 8945664 | tf_op jit(solution)/shard_map/reshape | solution.py:47
  235.9 46.4 %all-to-all-done.1 = bf16[91,96,256]{2,0,1:T(8,128)(2,1)} async-done(((bf16[91,96,256]{2,0,1:T(8,128)(2,1)}), bf16[91,96,256]{2,0,1:T(8,128)(2,1)}, u32[]{:S(2)}, u32[]{:S(2)}) %all-to-all-start.1) | async-done | bytes 4472864 | tf_op jit(solution)/shard_map/all_to_all | solution.py:48
  282.3 4.3 all-to-all-start.2
  286.7 0.1 reshape.207
  287.1 41.2 %fusion.11 = bf16[91,384,64]{1,0,2:T(8,128)(2,1)} fusion(pred[91]{0:T(512)(128)(4,1)S(1)} %add_compare_fusion, bf16[91,64,1440]{2,1,0:T(8,128)(2,1)} %param.7, s32[384]{0:T(512)S(1)} %mul.158, s32[384]{0:T(512)S(1)} %add.79), kind=kOutput, calls=%fused_computation.16 | convolution fusion | flops 6453669888 | bytes 21249116 | tf_op jit(solution)/shard_map/ack,kn->anc/dot_general | solution.py:45
  328.3 8.6 %copy.65 = bf16[91,384,64]{0,2,1:T(8,128)(2,1)} copy(bf16[91,384,64]{1,0,2:T(8,128)(2,1)} %fusion.11) | data formatting | bytes 8945664 | tf_op jit(solution)/shard_map/convert_element_type | solution.py:46
  336.9 8.3 %copy.66 = bf16[91,96,256]{2,0,1:T(8,128)(2,1)} copy(bf16[91,96,256]{0,2,1:T(8,128)(2,1)} %bitcast.83) | data formatting | bytes 8945664 | tf_op jit(solution)/shard_map/reshape | solution.py:47
  345.2 46.4 %all-to-all-done.2 = bf16[91,96,256]{2,0,1:T(8,128)(2,1)} async-done(((bf16[91,96,256]{2,0,1:T(8,128)(2,1)}), bf16[91,96,256]{2,0,1:T(8,128)(2,1)}, u32[]{:S(2)}, u32[]{:S(2)}) %all-to-all-start.2) | async-done | bytes 4472864 | tf_op jit(solution)/shard_map/all_to_all | solution.py:48
  391.6 4.1 all-to-all-start.3
  396.3 8.2 %copy.46 = bf16[32,91,3,256]{1,3,2,0:T(8,128)(2,1)} copy(bf16[32,91,3,256]{3,1,2,0:T(8,128)(2,1)} %bitcast.4) | data formatting | bytes 8945664 | tf_op jit(solution)/shard_map/all_to_all | solution.py:48
  404.6 18.3 %copy.47 = bf16[3,8,91,4,4,64]{2,1,5,4,3,0:T(8,128)(2,1)} copy(bf16[3,8,91,4,4,64]{2,5,3,0,4,1:T(8,128)(2,1)} %bitcast.76) | data formatting | bytes 8945664 | tf_op jit(solution)/shard_map/transpose | solution.py:50
  422.9 10.7 %reshape.217 = bf16[3,728,1024]{1,2,0:T(8,128)(2,1)} reshape(bf16[3,8,91,4,4,64]{2,1,5,4,3,0:T(8,128)(2,1)} %copy.47) | data formatting | bytes 8945664 | tf_op jit(solution)/shard_map/reshape | solution.py:51
  433.6 8.1 %copy.53 = bf16[32,91,3,256]{1,3,2,0:T(8,128)(2,1)} copy(bf16[32,91,3,256]{3,1,2,0:T(8,128)(2,1)} %bitcast.12) | data formatting | bytes 8945664 | tf_op jit(solution)/shard_map/all_to_all | solution.py:48
  441.6 18.1 %copy.54 = bf16[3,8,91,4,4,64]{2,1,5,4,3,0:T(8,128)(2,1)} copy(bf16[3,8,91,4,4,64]{2,5,3,0,4,1:T(8,128)(2,1)} %bitcast.77) | data formatting | bytes 8945664 | tf_op jit(solution)/shard_map/transpose | solution.py:50
  459.7 10.7 %reshape.219 = bf16[3,728,1024]{1,2,0:T(8,128)(2,1)} reshape(bf16[3,8,91,4,4,64]{2,1,5,4,3,0:T(8,128)(2,1)} %copy.54) | data formatting | bytes 8945664 | tf_op jit(solution)/shard_map/reshape | solution.py:51
  470.4 6.6 %fusion.24 = f32[3,721,1024]{2,1,0:T(8,128)S(1)} fusion(bf16[3,728,1024]{1,2,0:T(8,128)(2,1)} %reshape.217, bf16[12,721,728]{2,1,0:T(8,128)(2,1)} %param.8), kind=kOutput, calls=%fused_computation.33 | convolution fusion | flops 3224911872 | bytes 16932864 | tf_op jit(solution)/shard_map/brl,bln->brn/dot_general | solution.py:52
  477.0 6.6 %fusion.27 = f32[3,721,1024]{2,1,0:T(8,128)S(1)} fusion(bf16[3,728,1024]{1,2,0:T(8,128)(2,1)} %reshape.219, bf16[12,721,728]{2,1,0:T(8,128)(2,1)} %param.8), kind=kOutput, calls=%fused_computation.34 | convolution fusion | flops 3224911872 | bytes 16932864 | tf_op jit(solution)/shard_map/brl,bln->brn/dot_general | solution.py:52
  483.6 3.9 fusion.14
  487.5 6.4 %reshape.196 = f32[3,721,2,256]{3,2,1,0:T(2,128)} reshape(f32[3,721,512]{2,1,0:T(8,128)} %get-tuple-element.23) | data formatting | bytes 8859648 | tf_op jit(solution)/shard_map/reshape | solution.py:61
  493.9 6.4 %reshape.201 = f32[3,721,2,256]{3,2,1,0:T(2,128)} reshape(f32[3,721,512]{2,1,0:T(8,128)} %get-tuple-element.22) | data formatting | bytes 8859648 | tf_op jit(solution)/shard_map/reshape | solution.py:61
  500.2 8.2 %copy.60 = bf16[32,91,3,256]{1,3,2,0:T(8,128)(2,1)} copy(bf16[32,91,3,256]{3,1,2,0:T(8,128)(2,1)} %bitcast.20) | data formatting | bytes 8945664 | tf_op jit(solution)/shard_map/all_to_all | solution.py:48
  508.5 18.4 %copy.61 = bf16[3,8,91,4,4,64]{2,1,5,4,3,0:T(8,128)(2,1)} copy(bf16[3,8,91,4,4,64]{2,5,3,0,4,1:T(8,128)(2,1)} %bitcast.78) | data formatting | bytes 8945664 | tf_op jit(solution)/shard_map/transpose | solution.py:50
  526.9 10.7 %reshape.221 = bf16[3,728,1024]{1,2,0:T(8,128)(2,1)} reshape(bf16[3,8,91,4,4,64]{2,1,5,4,3,0:T(8,128)(2,1)} %copy.61) | data formatting | bytes 8945664 | tf_op jit(solution)/shard_map/reshape | solution.py:51
  537.5 10.5 %fusion.30 = f32[3,721,1024]{2,1,0:T(8,128)} fusion(bf16[3,728,1024]{1,2,0:T(8,128)(2,1)} %reshape.221, bf16[12,721,728]{2,1,0:T(8,128)(2,1)} %param.8), kind=kOutput, calls=%fused_computation.35 | convolution fusion | flops 3224911872 | bytes 16932864 | tf_op jit(solution)/shard_map/brl,bln->brn/dot_general | solution.py:52
  548.1 8.1 %copy.67 = bf16[32,91,3,256]{1,3,2,0:T(8,128)(2,1)} copy(bf16[32,91,3,256]{3,1,2,0:T(8,128)(2,1)} %bitcast.28) | data formatting | bytes 8945664 | tf_op jit(solution)/shard_map/all_to_all | solution.py:48
  556.1 18.1 %copy.68 = bf16[3,8,91,4,4,64]{2,1,5,4,3,0:T(8,128)(2,1)} copy(bf16[3,8,91,4,4,64]{2,5,3,0,4,1:T(8,128)(2,1)} %bitcast.79) | data formatting | bytes 8945664 | tf_op jit(solution)/shard_map/transpose | solution.py:50
  574.3 10.8 %reshape.223 = bf16[3,728,1024]{1,2,0:T(8,128)(2,1)} reshape(bf16[3,8,91,4,4,64]{2,1,5,4,3,0:T(8,128)(2,1)} %copy.68) | data formatting | bytes 8945664 | tf_op jit(solution)/shard_map/reshape | solution.py:51
  585.0 10.8 %fusion.33 = f32[3,721,1024]{2,1,0:T(8,128)} fusion(bf16[3,728,1024]{1,2,0:T(8,128)(2,1)} %reshape.223, bf16[12,721,728]{2,1,0:T(8,128)(2,1)} %param.8), kind=kOutput, calls=%fused_computation.36 | convolution fusion | flops 3224911872 | bytes 16932864 | tf_op jit(solution)/shard_map/brl,bln->brn/dot_general | solution.py:52
  595.8 8.4 %fusion.12 = (f32[3,721,512]{2,1,0:T(8,128)}, f32[3,721,512]{2,1,0:T(8,128)}) fusion(f32[3,721,1024]{2,1,0:T(8,128)} %fusion.33, f32[3]{0:T(128)S(1)} %get-tuple-element.17, pred[3,721]{1,0:T(4,128)(4,1)S(1)} %iota_compare_fusion, f32[3]{0:T(128)S(1)} %get-tuple-element.18, f32[3,721,1024]{2,1,0:T(8,128)S(1)} %bitcast.85, ...), kind=kLoop, calls=%fused_computation.18 | loop fusion | flops 4429824 | bytes 26583294 | tf_op jit(solution)/shard_map/mul | solution.py:60
  604.2 6.4 %reshape.206 = f32[3,721,2,256]{3,2,1,0:T(2,128)} reshape(f32[3,721,512]{2,1,0:T(8,128)} %get-tuple-element.21) | data formatting | bytes 8859648 | tf_op jit(solution)/shard_map/reshape | solution.py:61
  610.6 6.4 %reshape.211 = f32[3,721,2,256]{3,2,1,0:T(2,128)} reshape(f32[3,721,512]{2,1,0:T(8,128)} %get-tuple-element.20) | data formatting | bytes 8859648 | tf_op jit(solution)/shard_map/reshape | solution.py:61
  617.0 13.8 %pad_maximum_fusion = f32[12,721,2,256]{3,2,1,0:T(2,128)} fusion(f32[3,721,2,256]{3,2,1,0:T(2,128)} %reshape.211, f32[3,721,2,256]{3,2,1,0:T(2,128)} %reshape.206, f32[3,721,2,256]{3,2,1,0:T(2,128)} %reshape.201, f32[3,721,2,256]{3,2,1,0:T(2,128)} %reshape.196), kind=kLoop, calls=%fused_computation | loop fusion | flops 13289472 | bytes 35438592 | tf_op jit(solution)/shard_map/concatenate | solution.py:62
  (39 shorter events, 2.4 us)
Async XLA Ops:
  59.8 112.8 %all-to-all-start = ((bf16[91,96,256]{2,0,1:T(8,128)(2,1)}), bf16[91,96,256]{2,0,1:T(8,128)(2,1)}, u32[]{:S(2)}, u32[]{:S(2)}) async-start(bf16[91,96,256]{2,0,1:T(8,128)(2,1)} %copy.45), calls=%async_computation | async-start | bytes 9437184 | tf_op jit(solution)/shard_map/all_to_all | solution.py:48
  172.6 109.7 %all-to-all-start.1 = ((bf16[91,96,256]{2,0,1:T(8,128)(2,1)}), bf16[91,96,256]{2,0,1:T(8,128)(2,1)}, u32[]{:S(2)}, u32[]{:S(2)}) async-start(bf16[91,96,256]{2,0,1:T(8,128)(2,1)} %copy.52), calls=%async_computation.1 | async-start | bytes 9437184 | tf_op jit(solution)/shard_map/all_to_all | solution.py:48
  282.3 109.3 %all-to-all-start.2 = ((bf16[91,96,256]{2,0,1:T(8,128)(2,1)}), bf16[91,96,256]{2,0,1:T(8,128)(2,1)}, u32[]{:S(2)}, u32[]{:S(2)}) async-start(bf16[91,96,256]{2,0,1:T(8,128)(2,1)} %copy.59), calls=%async_computation.2 | async-start | bytes 9437184 | tf_op jit(solution)/shard_map/all_to_all | solution.py:48
  345.2 50.6 %copy-start = (s32[384]{0:T(512)S(1)}, s32[384]{0:T(512)}, u32[]{:S(2)}) copy-start(s32[384]{0:T(512)} %param.9) | copy-start | bytes 4612
  391.6 156.5 %all-to-all-start.3 = ((bf16[91,96,256]{2,0,1:T(8,128)(2,1)}), bf16[91,96,256]{2,0,1:T(8,128)(2,1)}, u32[]{:S(2)}, u32[]{:S(2)}) async-start(bf16[91,96,256]{2,0,1:T(8,128)(2,1)} %copy.66), calls=%async_computation.3 | async-start | bytes 9437184 | tf_op jit(solution)/shard_map/all_to_all | solution.py:48
  574.3 21.6 %slice-start = ((s8[8945664]{0:T(1024)(128)(4,1)}), s8[557056]{0:T(1024)(128)(4,1)S(1)}, s32[]{:S(2)}) async-start(s8[8945664]{0:T(1024)(128)(4,1)} %bitcast.84), calls=%async_computation.4 | async-start | bytes 1114112
  585.0 10.8 %slice-start.1 = ((s8[8945664]{0:T(1024)(128)(4,1)}), s8[4194304]{0:T(1024)(128)(4,1)S(1)}, s32[]{:S(2)}) async-start(s8[8945664]{0:T(1024)(128)(4,1)} %bitcast.84), calls=%async_computation.5 | async-start | bytes 8388608
  585.0 10.8 %slice-start.2 = ((s8[8945664]{0:T(1024)(128)(4,1)}), s8[4194304]{0:T(1024)(128)(4,1)S(1)}, s32[]{:S(2)}) async-start(s8[8945664]{0:T(1024)(128)(4,1)} %bitcast.84), calls=%async_computation.6 | async-start | bytes 8388608
where the time goes:
time: 641 us; the launch traced here: 631 us
  local copies, waits for them, and re-layouts  244 us (38%)
  matrix products  199 us (31%)
  waiting for transfers between devices  139 us (22%)
  other arithmetic  27.2 us (4%)
  starting transfers between devices  20.7 us (3%)
    dot_general x4, matrix products, per_device(): jnp.einsum('ack,kn->anc', field, basis, preferred_element_type=jnp.float32)  165 us
    all_to_all x4, waiting for transfers between devices, per_device(): lax.all_to_all(fourier, ('lat', 'ch'), split_axis=1, concat_axis=0, tiled...  139 us
    transpose x4, local copies, waits for them, and re-layouts, per_device(): got = got.transpose(3, 0, 2, 4, 1, 5)  72.9 us
    reshape x4, local copies, waits for them, and re-layouts, per_device(): got = got.reshape(width, lat_count * lat_rows, 4 * ch_count * chan_dev)  42.8 us
    dot_general x4, matrix products, per_device(): jnp.einsum('brl,bln->brn', legendre[g * width:(g + 1) * width], got, pref...  34.5 us
    convert_element_type x4, local copies, waits for them, and re-layouts, per_device(): fourier = jnp.where(in_grid, fourier * norm_scale, 0.0).astype(jnp.bfloat16)  34.4 us
    reshape x4, local copies, waits for them, and re-layouts, per_device(): fourier = fourier.reshape(lat_rows, dev_count * width, 4 * chan_dev)  33.2 us
    all_to_all x4, local copies, waits for them, and re-layouts, per_device(): lax.all_to_all(fourier, ('lat', 'ch'), split_axis=1, concat_axis=0, tiled...  32.6 us
  transfers between devices with their start and end apart: 4, of which 3 were waited for; matrix products, arithmetic and copies ran while one was open for 52% of the time, Pallas kernels for 0%

commit v1 on v0

v1 whole, which is shorter than its diff:
```python
import functools
import math

import jax
import jax.numpy as jnp
import numpy as np
from jax import lax
from jax.experimental import pallas as pl
from jax.experimental.pallas import tpu as pltpu
from jax.sharding import PartitionSpec as P

NLAT = 721
PER = 2
DB = 32
LANES = 128
MESH = pl.DeviceIdType.MESH


def up(x, m):
    return -(-x // m) * m


def cos_coeffs():
    cheb = np.polynomial.chebyshev.Chebyshev.interpolate(
        lambda u: np.cos(np.pi * np.sqrt(np.abs(u))), 8, domain=[0.0, 1.0]
    )
    return [float(c) for c in cheb.convert(kind=np.polynomial.Polynomial).coef]


def xor(a, b, count):
    total, bit = 0, 1
    while bit < count:
        total = total + ((a // bit + b // bit) % 2) * bit
        bit *= 2
    return total


class Sizes:
    def __init__(self, field_shape, leg_shape, lat_count, ch_count):
        self.rows, self.chan, self.lon = field_shape
        self.own, self.deg, self.latp = leg_shape
        self.nl, self.nc = lat_count, ch_count
        self.nd = lat_count * ch_count
        self.orders = self.deg - 1
        self.groups = self.own // PER
        self.blocks = self.nd // DB
        self.step = max(s for s in range(1, 17) if self.rows % s == 0)
        self.chunks = self.rows // self.step
        self.clen = self.step * self.chan
        self.cpad = up(self.clen, LANES)
        self.pair = 2 * self.rows
        self.zrows = up(PER * self.pair, 16)
        self.start = [(b * self.pair) // 16 * 16 for b in range(PER)]
        self.win = max(
            [up((b + 1) * self.pair - self.start[b], 16) for b in range(PER)]
        )
        self.start = [min(s, self.zrows - self.win) for s in self.start]
        self.depth = self.nl * self.win
        self.ct = self.nc * self.chan // LANES
        self.per_row = 2 * self.ct
        self.orows = PER * self.deg * self.per_row


def kernel(
    z, field, leg, mcol, marks, bounds, out,
    fbuf, basis, zbuf, send, recv, sel, pbuf, obuf,
    fsem, psem, osem, send_sem, recv_sem,
):
    lat = lax.axis_index("lat")
    ch = lax.axis_index("ch")
    me = lat * z.nc + ch
    poly = cos_coeffs()
    scale = 2.0 * math.pi / z.lon
    total_steps = z.groups * z.chunks
    lane = lax.broadcasted_iota(jnp.int32, (1, LANES), 1)
    low = lane < LANES // 2

    def field_copy(n, slot):
        c = lax.rem(n, z.chunks)
        src = field.at[pl.ds(pl.multiple_of(c * z.clen, 16), z.clen)]
        return pltpu.make_async_copy(src, fbuf.at[slot, pl.ds(0, z.clen)], fsem.at[slot])

    field_copy(0, 0).start()

    def build_basis(g, blk):
        def one(s, _):
            m = mcol[g, pl.ds(pl.multiple_of(blk * 8 * DB + s * 16, 16), 16), :]
            phase = ((s // 2) % 2) * (z.lon // 4)
            k = lax.broadcasted_iota(jnp.int32, (16, z.lon), 1).astype(jnp.float32)
            x = m * k + phase.astype(jnp.float32)
            r = x - z.lon * jnp.floor(x * (1.0 / z.lon) + 0.5)
            r = r * (2.0 / z.lon)
            u = r * r
            acc = jnp.full_like(u, poly[-1])
            for c in poly[-2::-1]:
                acc = acc * u + c
            basis[blk, pl.ds(pl.multiple_of(s * 16, 16), 16), :] = acc.astype(jnp.bfloat16)
            return 0

        lax.fori_loop(0, 8 * DB // 16, one, 0)

    def transform(g):
        def chunk(c, _):
            n = g * z.chunks + c
            slot = lax.rem(n, 2)

            @pl.when(n + 1 < total_steps)
            def _():
                field_copy(n + 1, lax.rem(n + 1, 2)).start()

            @pl.when(c == 0)
            def _():
                lax.fori_loop(0, z.blocks, lambda blk, _: (build_basis(g, blk), 0)[1], 0)

            field_copy(n, slot).wait()

            def block(blk, _):
                ft = lax.dot_general(
                    basis[blk], fbuf[slot], (((1,), (1,)), ((), ())),
                    preferred_element_type=jnp.float32,
                )
                for s in range(2 * PER):
                    re = ft[2 * s * DB : (2 * s + 1) * DB]
                    im = ft[(2 * s + 1) * DB : (2 * s + 2) * DB]
                    for j in range(z.cpad // LANES):
                        v0 = re[:, j * LANES : (j + 1) * LANES]
                        v1 = im[:, j * LANES : (j + 1) * LANES]
                        base = blk * DB * z.zrows + s * z.rows + c * z.step + 2 * j
                        even = jnp.where(low, v0, pltpu.roll(v1, LANES // 2, 1))
                        zbuf[pl.ds(base, DB, stride=z.zrows), :] = even
                        if 2 * j + 1 < z.step:
                            odd = jnp.where(low, pltpu.roll(v0, LANES // 2, 1), v1)
                            zbuf[pl.ds(base + 1, DB, stride=z.zrows), :] = odd
                return 0

            lax.fori_loop(0, z.blocks, block, 0)
            return 0

        lax.fori_loop(0, z.chunks, chunk, 0)

    def all_sent(slot):
        ref = send.at[slot, pl.ds(0, z.nd - 1)]
        return pltpu.make_async_copy(ref, ref, send_sem.at[slot])

    def all_here(g):
        ref = send.at[0, pl.ds(0, z.nd - 1)]
        return pltpu.make_async_copy(ref, ref, recv_sem.at[g])

    def pack_and_send(g):
        slot = lax.rem(g, 2)

        def pack(d, _):
            rows = zbuf[pl.ds(pl.multiple_of(d * z.zrows, 16), z.zrows), :]
            send[slot, d] = (rows * scale).astype(jnp.bfloat16)
            return 0

        lax.fori_loop(0, z.nd, pack, 0)

        def issue(n, _):
            d = xor(me, z.nd - 1 - n, z.nd)
            pltpu.make_async_remote_copy(
                src_ref=send.at[slot, d],
                dst_ref=recv.at[g, lat, ch],
                send_sem=send_sem.at[slot],
                recv_sem=recv_sem.at[g],
                device_id=(d // z.nc, d % z.nc),
                device_id_type=MESH,
            ).start()
            return 0

        lax.fori_loop(0, z.nd - 1, issue, 0)
        recv[g, lat, ch] = send[slot, me]

    def leg_copy(g, b):
        return pltpu.make_async_copy(leg.at[g * PER + b], pbuf.at[b], psem.at[b])

    def build_select():
        step = max(s for s in range(8, 129, 8) if z.latp % s == 0)
        for b in range(PER):
            target = marks[b, 0:1, :]

            def one(n, _):
                at = pl.multiple_of(n * step, 8)
                row = lax.broadcasted_iota(jnp.int32, (step, 1), 0) + at
                hit = jnp.where(row == target, 1.0, 0.0).astype(jnp.bfloat16)
                sel[b, pl.ds(at, step), :] = hit
                return 0

            lax.fori_loop(0, z.latp // step, one, 0)

    cuts = [0, 240, 480, z.deg]

    def out_copy(g):
        dst = out.at[pl.ds(pl.multiple_of(g * z.orows, 8), z.orows)]
        return pltpu.make_async_copy(obuf, dst, osem)

    def legendre(g):
        all_here(g).wait()
        for b in range(PER):
            leg_copy(g, b).wait()
            first = bounds[0, g * PER + b]
            second = bounds[1, g * PER + b]
            in_first = marks[b, 1:2, :] == 0
            at = z.start[b]
            rhs = jnp.concatenate(
                [
                    recv[g, :, j, at : at + z.win, :].reshape(z.depth, LANES)
                    for j in range(z.nc)
                ],
                axis=1,
            )
            for lo, hi in zip(cuts[:-1], cuts[1:]):
                spread = jnp.dot(
                    pbuf[b, lo:hi, :], sel[b], preferred_element_type=jnp.float32
                )
                r = lax.broadcasted_iota(jnp.int32, (hi - lo, 1), 0) + lo
                upper = jnp.where(r < first, 1.0, 0.0)
                lower = jnp.where(r >= second, 1.0, 0.0)
                mask = jnp.where(in_first, upper, lower)
                lhs = (spread * mask).astype(jnp.bfloat16)
                y = jnp.dot(lhs, rhs, preferred_element_type=jnp.float32)
                for t in range(z.ct):
                    p0 = y[:, 2 * t * LANES : (2 * t + 1) * LANES]
                    p1 = y[:, (2 * t + 1) * LANES : (2 * t + 2) * LANES]
                    re = jnp.where(low, p0, pltpu.roll(p1, LANES // 2, 1))
                    im = jnp.where(low, pltpu.roll(p0, LANES // 2, 1), p1)
                    base = (b * z.deg + lo) * z.per_row + 2 * t
                    obuf[pl.ds(base, hi - lo, stride=z.per_row), :] = re
                    obuf[pl.ds(base + 1, hi - lo, stride=z.per_row), :] = im
        out_copy(g).start()
        out_copy(g).wait()

    def body(g, _):
        @pl.when(g < z.groups)
        def _():
            @pl.when(g == 0)
            def _():
                zbuf[...] = jnp.zeros_like(zbuf)

            transform(g)

            @pl.when(g >= 2)
            def _():
                all_sent(lax.rem(g, 2)).wait()

            pack_and_send(g)

            @pl.when(g == 0)
            def _():
                build_select()

        @pl.when(g >= 2)
        def _():
            for b in range(PER):
                leg_copy(g - 2, b).start()
            legendre(g - 2)

        return 0

    lax.fori_loop(0, z.groups + 2, body, 0)
    for g in range(max(z.groups - 2, 0), z.groups):
        all_sent(g % 2).wait()


def per_device(field, legendre, pair_order):
    z = Sizes(
        field.shape, legendre.shape, lax.axis_size("lat"), lax.axis_size("ch")
    )
    me = lax.axis_index("lat") * z.nc + lax.axis_index("ch")
    keep = pair_order < z.orders // 2
    first = jnp.where(keep, pair_order, 0)
    both = jnp.stack([first, z.orders - 1 - first], axis=1)
    cols = both.reshape(z.blocks, DB, z.groups, PER, 2).transpose(2, 0, 3, 4, 1)
    cols = jnp.broadcast_to(cols[:, :, :, :, None, :], cols.shape[:4] + (2, DB))
    mcol = cols.reshape(z.groups, z.blocks * 8 * DB, 1).astype(jnp.float32)
    far = 4 * z.deg
    lims = jnp.stack(
        [jnp.where(keep, z.orders - first, 0), jnp.where(keep, z.orders - first, far)]
    )
    bounds = lax.dynamic_slice_in_dim(lims, me * z.own, z.own, axis=1)

    col = np.arange(z.depth)
    marks = np.zeros((PER, 8, z.depth), np.int32)
    for b in range(PER):
        u = col % z.win - (b * z.pair - z.start[b])
        lat = (col // z.win) * z.rows + u % z.rows
        ok = (u >= 0) & (u < z.pair) & (lat < NLAT)
        marks[b, 0] = np.where(ok, lat, -1)
        marks[b, 1] = (u // z.rows) % 2

    bf, f32 = jnp.bfloat16, jnp.float32
    vmem = pl.BlockSpec(memory_space=pltpu.VMEM)
    hbm = pl.BlockSpec(memory_space=pl.ANY)
    dma = pltpu.SemaphoreType.DMA
    flat = pl.pallas_call(
        functools.partial(kernel, z),
        out_shape=jax.ShapeDtypeStruct((z.groups * z.orows, LANES), f32),
        in_specs=[hbm, hbm, vmem, vmem, pl.BlockSpec(memory_space=pltpu.SMEM)],
        out_specs=hbm,
        scratch_shapes=[
            pltpu.VMEM((2, z.cpad, z.lon), bf),
            pltpu.VMEM((z.blocks, 8 * DB, z.lon), bf),
            pltpu.VMEM((z.nd * z.zrows, LANES), f32),
            pltpu.VMEM((2, z.nd, z.zrows, LANES), bf),
            pltpu.VMEM((z.groups, z.nl, z.nc, z.zrows, LANES), bf),
            pltpu.VMEM((PER, z.latp, z.depth), bf),
            pltpu.VMEM((PER, z.deg, z.latp), bf),
            pltpu.VMEM((z.orows, LANES), f32),
            dma((2,)), dma((PER,)), dma, dma((2,)), dma((z.groups,)),
        ],
        compiler_params=pltpu.CompilerParams(
            has_side_effects=True, vmem_limit_bytes=67043328
        ),
    )(
        field.reshape(z.rows * z.chan, z.lon), legendre, mcol, jnp.asarray(marks), bounds
    )
    shaped = flat.reshape(z.own, z.deg, z.ct, 2, LANES).transpose(0, 1, 3, 2, 4)
    return shaped.reshape(z.own, z.deg, 2, z.ct * LANES)


def solution(mesh):
    in_specs = (P("lat", "ch", None), P(("lat", "ch"), None, None), P())
    out_specs = P(("lat", "ch"), None, None, None)
    return jax.shard_map(
        per_device, mesh=mesh, in_specs=in_specs, out_specs=out_specs, check_vma=False
    )
```

time: 641 us -> 467 us (0.73); the launches traced: 631 us -> 466 us
  Pallas kernels: 0 us -> 450 us
  local copies, waits for them, and re-layouts: 244 us -> 14.6 us
  matrix products: 199 us -> 0 us
  waiting for transfers between devices: 139 us -> 0 us
  other arithmetic: 27.2 us -> 1.36 us
  starting transfers between devices: 20.7 us -> 0 us
    pallas_call x0 -> x1, Pallas kernels: none -> 450 us  [per_device(): pl.pallas_call(functools.partial(kernel, z), out_shape=jax.ShapeDtypeStru...]
    dot_general x8 -> x0, matrix products: 199 us -> none  [the longest x4 165 us: per_device(): jnp.einsum('ack,kn->anc', field, basis, preferred_element_type=jnp.float32)]
    all_to_all x4 -> x0, waiting for transfers between devices: 139 us -> none  [per_device(): lax.all_to_all(fourier, ('lat', 'ch'), split_axis=1, concat_axis=0, tiled...]
    reshape x16 -> x0, local copies, waits for them, and re-layouts: 102 us -> none  [the longest x4 42.8 us: per_device(): got = got.reshape(width, lat_count * lat_rows, 4 * ch_count * chan_dev)]
    transpose x4 -> x0, local copies, waits for them, and re-layouts: 72.9 us -> none  [per_device(): got = got.transpose(3, 0, 2, 4, 1, 5)]
    convert_element_type x4 -> x1, local copies, waits for them, and re-layouts: 34.4 us -> 1.69 us  [per_device(): mcol = cols.reshape(z.groups, z.blocks * 8 * DB, 1).astype(jnp.float32)]
    all_to_all x4 -> x0, local copies, waits for them, and re-layouts: 32.6 us -> none  [per_device(): lax.all_to_all(fourier, ('lat', 'ch'), split_axis=1, concat_axis=0, tiled...]
    all_to_all x4 -> x0, starting transfers between devices: 20.7 us -> none  [per_device(): lax.all_to_all(fourier, ('lat', 'ch'), split_axis=1, concat_axis=0, tiled...]
  transfers between devices with their start and end apart: 4 -> 0, of which waited for: 3 -> 0; matrix products, arithmetic and copies ran while one was open for 52% -> 0% of each run, Pallas kernels for 0% -> 0%
where the time goes in v1:
time: 467 us; the launch traced here: 466 us
  Pallas kernels  450 us (96%)
  local copies, waits for them, and re-layouts  14.6 us (3%)
    pallas_call x1, Pallas kernels, per_device(): pl.pallas_call(functools.partial(kernel, z), out_shape=jax.ShapeDtypeStru...  450 us
    unnamed x1, local copies, waits for them, and re-layouts  12.4 us

profile of v1, /device:TPU:0, one launch (start us, length us, event | category | flops | bytes accessed | tf_op | source)
XLA Modules:
  0.0 466.5 jit_solution(15503387648669934372)
XLA Ops:
  0.0 0.7 subtract_select_fusion
  0.7 0.7 fusion.1.bounds
  1.3 0.1 stack.19
  1.5 0.1 copy.10
  1.6 0.1 stack.18
  1.8 0.1 copy.9
  1.9 1.7 convert_element_type.13.mcol
  3.6 450.5 %shard_map.46 = f32[34608,128]{1,0:T(8,128)} custom-call(bf16[5824,1440]{1,0:T(8,128)(2,1)} %bitcast.11, bf16[12,721,728]{2,1,0:T(8,128)(2,1)} %leg.1, f32[6,256,1]{2,1,0:T(8,128)} %convert_element_type.13.mcol, s32[2,8,1536]{2,1,0:T(8,128)} %constant.27.clone.marks, s32[2,12]{1,0:T(2,128)} %fusion.1.bounds), custom_call_target="tpu_custom_call" | custom-call | tf_op jit(solution)/shard_map/pallas_call | solution.py:295
  454.1 12.4 %copy.14 = f32[12,721,2,256]{3,2,1,0:T(2,128)} copy(f32[12,721,2,256]{3,2,1,0:T(2,128)} %bitcast.10) | data formatting | bytes 35438592
  (4 shorter events, 0.0 us)

commit v2 on v1

v2 whole, which is shorter than its diff:
```python
import functools
import math

import jax
import jax.numpy as jnp
import numpy as np
from jax import lax
from jax.experimental import pallas as pl
from jax.experimental.pallas import tpu as pltpu
from jax.sharding import PartitionSpec as P

NLAT = 721
PER = 2
DB = 32
LANES = 128
MESH = pl.DeviceIdType.MESH


def up(x, m):
    return -(-x // m) * m


def cos_coeffs():
    cheb = np.polynomial.chebyshev.Chebyshev.interpolate(
        lambda u: np.cos(np.pi * np.sqrt(np.abs(u))), 8, domain=[0.0, 1.0]
    )
    return [float(c) for c in cheb.convert(kind=np.polynomial.Polynomial).coef]


def xor(a, b, count):
    total, bit = 0, 1
    while bit < count:
        total = total + ((a // bit + b // bit) % 2) * bit
        bit *= 2
    return total


class Sizes:
    def __init__(self, field_shape, leg_shape, lat_count, ch_count):
        self.rows, self.chan, self.lon = field_shape
        self.own, self.deg, self.latp = leg_shape
        self.nl, self.nc = lat_count, ch_count
        self.nd = lat_count * ch_count
        self.orders = self.deg - 1
        self.groups = self.own // PER
        self.blocks = self.nd // DB
        self.step = max(s for s in range(1, 9) if self.rows % s == 0)
        self.chunks = self.rows // self.step
        self.clen = self.step * self.chan
        self.cpad = up(self.clen, LANES)
        self.pair = 2 * self.rows
        self.zrows = up(PER * self.pair, 16)
        self.start = [(b * self.pair) // 16 * 16 for b in range(PER)]
        self.win = max(
            [up((b + 1) * self.pair - self.start[b], 16) for b in range(PER)]
        )
        self.start = [min(s, self.zrows - self.win) for s in self.start]
        self.depth = self.nl * self.win
        mid = up(self.zrows // 2, 16)
        self.pieces = [(0, mid), (mid, self.zrows - mid)]
        self.ct = self.nc * self.chan // LANES
        self.per_row = 2 * self.ct
        self.orows = PER * self.deg * self.per_row


def kernel(
    z, field, leg, mrow, marks, bounds, out,
    fbuf, basis, zbuf, send, recv, sel, pbuf, lhs,
    fsem, psem, send_sem, recv_sem,
):
    lat = lax.axis_index("lat")
    ch = lax.axis_index("ch")
    me = lat * z.nc + ch
    poly = cos_coeffs()
    scale = 2.0 * math.pi / z.lon
    total_steps = z.groups * z.chunks
    lane = lax.broadcasted_iota(jnp.int32, (1, LANES), 1)
    low = lane < LANES // 2

    def field_copy(n, slot):
        c = lax.rem(n, z.chunks)
        src = field.at[pl.ds(pl.multiple_of(c * z.clen, 16), z.clen)]
        return pltpu.make_async_copy(src, fbuf.at[slot, pl.ds(0, z.clen)], fsem.at[slot])

    field_copy(0, 0).start()

    def partner(n):
        i = n // 2
        t = z.nd - 1 - i // 2 - (z.nd // 4) * (i % 2) - (z.nd // 2) * (n % 2)
        return xor(me, t, z.nd)

    barrier = pltpu.get_barrier_semaphore()

    def greet(n, _):
        d = partner(n)
        pl.semaphore_signal(
            barrier, inc=1, device_id=(d // z.nc, d % z.nc), device_id_type=MESH
        )
        return 0

    lax.fori_loop(0, z.nd - 1, greet, 0)

    tall = max(s for s in range(16, 97, 16) if z.lon % s == 0)

    def build_basis(g, blk):
        at = pl.multiple_of(blk * 8 * DB, LANES)
        m = mrow[g, 0:1, pl.ds(at, 8 * DB)]
        phase = mrow[g, 1:2, pl.ds(at, 8 * DB)]

        def one(s, _):
            top = pl.multiple_of(s * tall, 16)
            k = lax.broadcasted_iota(jnp.int32, (tall, 8 * DB), 0) + top
            x = m * k.astype(jnp.float32) + phase
            r = x - z.lon * jnp.floor(x * (1.0 / z.lon) + 0.5)
            r = r * (2.0 / z.lon)
            u = r * r
            acc = jnp.full_like(u, poly[-1])
            for c in poly[-2::-1]:
                acc = acc * u + c
            basis[blk, pl.ds(top, tall), :] = acc.astype(jnp.bfloat16)
            return 0

        lax.fori_loop(0, z.lon // tall, one, 0)

    def transform(g):
        def chunk(c, _):
            n = g * z.chunks + c
            slot = lax.rem(n, 2)

            @pl.when(n + 1 < total_steps)
            def _():
                field_copy(n + 1, lax.rem(n + 1, 2)).start()

            @pl.when(c == 0)
            def _():
                lax.fori_loop(0, z.blocks, lambda blk, _: (build_basis(g, blk), 0)[1], 0)

            field_copy(n, slot).wait()

            def block(blk, _):
                ft = jnp.dot(fbuf[slot], basis[blk], preferred_element_type=jnp.float32)
                for j in range(z.cpad // LANES):
                    turned = jnp.transpose(ft[j * LANES : (j + 1) * LANES])
                    for s in range(2 * PER):
                        v0 = turned[2 * s * DB : (2 * s + 1) * DB]
                        v1 = turned[(2 * s + 1) * DB : (2 * s + 2) * DB]
                        base = blk * DB * z.zrows + s * z.rows + c * z.step + 2 * j
                        even = jnp.where(low, v0, pltpu.roll(v1, LANES // 2, 1))
                        zbuf[pl.ds(base, DB, stride=z.zrows), :] = even
                        if 2 * j + 1 < z.step:
                            odd = jnp.where(low, pltpu.roll(v0, LANES // 2, 1), v1)
                            zbuf[pl.ds(base + 1, DB, stride=z.zrows), :] = odd
                return 0

            lax.fori_loop(0, z.blocks, block, 0)
            return 0

        lax.fori_loop(0, z.chunks, chunk, 0)

    def clear_pads():
        def one(d, _):
            at = pl.multiple_of((d + 1) * z.zrows - 16, 16)
            zbuf[pl.ds(at, 16), :] = jnp.zeros((16, LANES), jnp.float32)
            return 0

        lax.fori_loop(0, z.nd, one, 0)

    def all_sent(slot):
        ref = send.at[slot, pl.ds(0, z.nd - 1)]
        return pltpu.make_async_copy(ref, ref, send_sem.at[slot])

    def all_here(g, piece):
        ref = send.at[0, pl.ds(0, z.nd - 1), pl.ds(*z.pieces[piece])]
        return pltpu.make_async_copy(ref, ref, recv_sem.at[g, piece])

    def pack(g):
        slot = lax.rem(g, 2)

        def one(d, _):
            rows = zbuf[pl.ds(pl.multiple_of(d * z.zrows, 16), z.zrows), :]
            send[slot, d] = (rows * scale).astype(jnp.bfloat16)
            return 0

        lax.fori_loop(0, z.nd, one, 0)

    def ship(g):
        slot = lax.rem(g, 2)
        for piece, (at, size) in enumerate(z.pieces):

            def issue(n, _):
                d = partner(n)
                pltpu.make_async_remote_copy(
                    src_ref=send.at[slot, d, pl.ds(at, size)],
                    dst_ref=recv.at[g, lat, ch, pl.ds(at, size)],
                    send_sem=send_sem.at[slot],
                    recv_sem=recv_sem.at[g, piece],
                    device_id=(d // z.nc, d % z.nc),
                    device_id_type=MESH,
                ).start()
                return 0

            lax.fori_loop(0, z.nd - 1, issue, 0)
        recv[g, lat, ch] = send[slot, me]

    def leg_copy(g, b):
        return pltpu.make_async_copy(leg.at[g * PER + b], pbuf, psem)

    tile = max(s for s in range(8, 129, 8) if z.latp % s == 0)

    def build_select(b):
        target = marks[b, 0:1, :]

        def one(n, _):
            at = pl.multiple_of(n * tile, 8)
            row = lax.broadcasted_iota(jnp.int32, (tile, 1), 0) + at
            hit = jnp.where(row == target, 1.0, 0.0).astype(jnp.bfloat16)
            sel[pl.ds(at, tile), :] = hit
            return 0

        lax.fori_loop(0, z.latp // tile, one, 0)

    cuts = [0, 240, 480, z.deg]
    spans = list(zip(cuts[:-1], cuts[1:]))

    def left_factor(g, b):
        build_select(b)
        leg_copy(g, b).wait()
        first = bounds[0, g * PER + b]
        second = bounds[1, g * PER + b]
        in_first = marks[b, 1:2, :] == 0
        for lo, hi in spans:
            spread = jnp.dot(pbuf[lo:hi, :], sel[...], preferred_element_type=jnp.float32)
            r = lax.broadcasted_iota(jnp.int32, (hi - lo, 1), 0) + lo
            upper = jnp.where(r < first, 1.0, 0.0)
            lower = jnp.where(r >= second, 1.0, 0.0)
            mask = jnp.where(in_first, upper, lower)
            lhs[b, lo:hi, :] = (spread * mask).astype(jnp.bfloat16)

    def product(g, b):
        at = z.start[b]
        rhs = jnp.concatenate(
            [
                recv[g, :, j, at : at + z.win, :].reshape(z.depth, LANES)
                for j in range(z.nc)
            ],
            axis=1,
        )
        for lo, hi in spans:
            y = jnp.dot(lhs[b, lo:hi, :], rhs, preferred_element_type=jnp.float32)
            for t in range(z.ct):
                p0 = y[:, 2 * t * LANES : (2 * t + 1) * LANES]
                p1 = y[:, (2 * t + 1) * LANES : (2 * t + 2) * LANES]
                re = jnp.where(low, p0, pltpu.roll(p1, LANES // 2, 1))
                im = jnp.where(low, pltpu.roll(p0, LANES // 2, 1), p1)
                base = g * z.orows + (b * z.deg + lo) * z.per_row + 2 * t
                out[pl.ds(base, hi - lo, stride=z.per_row), :] = re
                out[pl.ds(base + 1, hi - lo, stride=z.per_row), :] = im

    def body(g, _):
        @pl.when(g < z.groups)
        def _():
            @pl.when(g == 0)
            def _():
                clear_pads()

            transform(g)

            @pl.when(g >= 2)
            def _():
                all_sent(lax.rem(g, 2)).wait()

            pack(g)

            @pl.when(g == 0)
            def _():
                pl.semaphore_wait(barrier, z.nd - 1)

            ship(g)

        @pl.when(g >= 2)
        def _():
            for b in range(PER):
                leg_copy(g - 2, b).start()
                left_factor(g - 2, b)
            for b in range(PER):
                all_here(g - 2, b).wait()
                product(g - 2, b)

        return 0

    lax.fori_loop(0, z.groups + 2, body, 0)
    for g in range(max(z.groups - 2, 0), z.groups):
        all_sent(g % 2).wait()


def per_device(field, legendre, pair_order):
    z = Sizes(
        field.shape, legendre.shape, lax.axis_size("lat"), lax.axis_size("ch")
    )
    me = lax.axis_index("lat") * z.nc + lax.axis_index("ch")
    keep = pair_order < z.orders // 2
    first = jnp.where(keep, pair_order, 0)
    both = jnp.stack([first, z.orders - 1 - first], axis=1)
    cols = both.reshape(z.blocks, DB, z.groups, PER, 2).transpose(2, 0, 3, 4, 1)
    cols = jnp.broadcast_to(cols[:, :, :, :, None, :], cols.shape[:4] + (2, DB))
    cols = cols.reshape(z.groups, z.blocks * 8 * DB).astype(jnp.float32)
    turn = np.arange(z.blocks * 8 * DB) // DB % 2 * (z.lon // 4)
    turn = jnp.broadcast_to(jnp.asarray(turn, jnp.float32), cols.shape)
    mrow = jnp.stack([cols, turn], axis=1)
    far = 4 * z.deg
    lims = jnp.stack(
        [jnp.where(keep, z.orders - first, 0), jnp.where(keep, z.orders - first, far)]
    )
    bounds = lax.dynamic_slice_in_dim(lims, me * z.own, z.own, axis=1)

    col = np.arange(z.depth)
    marks = np.zeros((PER, 8, z.depth), np.int32)
    for b in range(PER):
        u = col % z.win - (b * z.pair - z.start[b])
        lat = (col // z.win) * z.rows + u % z.rows
        ok = (u >= 0) & (u < z.pair) & (lat < NLAT)
        marks[b, 0] = np.where(ok, lat, -1)
        marks[b, 1] = (u // z.rows) % 2

    bf, f32 = jnp.bfloat16, jnp.float32
    vmem = pl.BlockSpec(memory_space=pltpu.VMEM)
    hbm = pl.BlockSpec(memory_space=pl.ANY)
    dma = pltpu.SemaphoreType.DMA
    flat = pl.pallas_call(
        functools.partial(kernel, z),
        out_shape=pltpu.VMEM((z.groups * z.orows, LANES), f32),
        in_specs=[hbm, hbm, vmem, vmem, pl.BlockSpec(memory_space=pltpu.SMEM)],
        out_specs=vmem,
        scratch_shapes=[
            pltpu.VMEM((2, z.cpad, z.lon), bf),
            pltpu.VMEM((z.blocks, z.lon, 8 * DB), bf),
            pltpu.VMEM((z.nd * z.zrows, LANES), f32),
            pltpu.VMEM((2, z.nd, z.zrows, LANES), bf),
            pltpu.VMEM((z.groups, z.nl, z.nc, z.zrows, LANES), bf),
            pltpu.VMEM((z.latp, z.depth), bf),
            pltpu.VMEM((z.deg, z.latp), bf),
            pltpu.VMEM((PER, z.deg, z.depth), bf),
            dma((2,)), dma, dma((2,)), dma((z.groups, len(z.pieces))),
        ],
        compiler_params=pltpu.CompilerParams(
            collective_id=0, has_side_effects=True, vmem_limit_bytes=67043328 - 4 * LANES * z.groups * z.orows - (1 << 19)
        ),
    )(
        field.reshape(z.rows * z.chan, z.lon), legendre, mrow, jnp.asarray(marks), bounds
    )
    shaped = flat.reshape(z.own, z.deg, z.ct, 2, LANES).transpose(0, 1, 3, 2, 4)
    return shaped.reshape(z.own, z.deg, 2, z.ct * LANES)


def solution(mesh):
    in_specs = (P("lat", "ch", None), P(("lat", "ch"), None, None), P())
    out_specs = P(("lat", "ch"), None, None, None)
    return jax.shard_map(
        per_device, mesh=mesh, in_specs=in_specs, out_specs=out_specs, check_vma=False
    )
```

time: 467 us -> 427 us (0.914)
  Pallas kernels: 450 us -> 415 us
  local copies, waits for them, and re-layouts: 14.6 us -> 7.77 us
    pallas_call x1, Pallas kernels: 450 us -> 415 us  [per_device(): pl.pallas_call(functools.partial(kernel, z), out_shape=pltpu.VMEM((z.grou...]
    unnamed x1, local copies, waits for them, and re-layouts: 12.4 us -> 6.47 us
where the time goes in v2:
time: 427 us; the launch traced here: 425 us
  Pallas kernels  415 us (97%)
  local copies, waits for them, and re-layouts  7.77 us (2%)
    pallas_call x1, Pallas kernels, per_device(): pl.pallas_call(functools.partial(kernel, z), out_shape=pltpu.VMEM((z.grou...  415 us

profile of v2, /device:TPU:0, one launch (start us, length us, event | category | flops | bytes accessed | tf_op | source)
XLA Modules:
  0.0 424.6 jit_solution(11769124103796484364)
XLA Ops:
  0.0 0.7 subtract_select_fusion
  0.7 0.6 fusion.1.bounds
  1.3 0.1 stack.23
  1.5 0.1 copy.10
  1.6 0.1 stack.22
  1.7 0.1 copy.9
  1.9 0.1 convert_element_type.23
  2.0 0.7 stack_broadcast_in_dim.3
  2.7 0.6 pad_maximum_fusion.mrow
  3.3 414.8 %shard_map.55 = f32[34608,128]{1,0:T(8,128)S(1)} custom-call(bf16[5824,1440]{1,0:T(8,128)(2,1)} %bitcast.11, bf16[12,721,728]{2,1,0:T(8,128)(2,1)} %leg.1, f32[6,2,256]{2,1,0:T(2,128)} %pad_maximum_fusion.mrow, s32[2,8,1536]{2,1,0:T(8,128)} %constant.30.clone.marks, s32[2,12]{1,0:T(2,128)} %fusion.1.bounds), custom_call_target="tpu_custom_call" | custom-call | tf_op jit(solution)/shard_map/pallas_call | solution.py:329
  418.1 6.5 %copy.13 = f32[12,721,2,256]{3,2,1,0:T(2,128)} copy(f32[12,721,2,256]{3,2,1,0:T(2,128)S(1)} %bitcast.10) | data formatting | bytes 35438592
  (4 shorter events, 0.0 us)

commit v3 on v2

--- a/solution.py
+++ b/solution.py
@@ -12,6 +12,8 @@
 NLAT = 721
 PER = 2
 DB = 32
+SLOTS = 3
+STEP = 13
 LANES = 128
 MESH = pl.DeviceIdType.MESH
 
@@ -44,7 +46,7 @@
         self.orders = self.deg - 1
         self.groups = self.own // PER
         self.blocks = self.nd // DB
-        self.step = max(s for s in range(1, 9) if self.rows % s == 0)
+        self.step = max(s for s in range(1, STEP + 1) if self.rows % s == 0)
         self.chunks = self.rows // self.step
         self.clen = self.step * self.chan
         self.cpad = up(self.clen, LANES)
@@ -58,13 +60,18 @@
         self.depth = self.nl * self.win
         mid = up(self.zrows // 2, 16)
         self.pieces = [(0, mid), (mid, self.zrows - mid)]
+        self.sends = []
+        for piece, (at, size) in enumerate(self.pieces):
+            part = up(size, 32) // 2
+            self.sends += [(piece, at, part), (piece, at + part, size - part)]
+        self.sends = [send for send in self.sends if send[2] > 0]
         self.ct = self.nc * self.chan // LANES
         self.per_row = 2 * self.ct
         self.orows = PER * self.deg * self.per_row
 
 
 def kernel(
-    z, field, leg, mrow, marks, bounds, out,
+    z, field, leg, held, marks, order, out,
     fbuf, basis, zbuf, send, recv, sel, pbuf, lhs,
     fsem, psem, send_sem, recv_sem,
 ):
@@ -82,7 +89,8 @@
         src = field.at[pl.ds(pl.multiple_of(c * z.clen, 16), z.clen)]
         return pltpu.make_async_copy(src, fbuf.at[slot, pl.ds(0, z.clen)], fsem.at[slot])
 
-    field_copy(0, 0).start()
+    for n in range(min(SLOTS - 1, total_steps)):
+        field_copy(n, n).start()
 
     def partner(n):
         i = n // 2
@@ -104,8 +112,12 @@
 
     def build_basis(g, blk):
         at = pl.multiple_of(blk * 8 * DB, LANES)
-        m = mrow[g, 0:1, pl.ds(at, 8 * DB)]
-        phase = mrow[g, 1:2, pl.ds(at, 8 * DB)]
+        col = lax.broadcasted_iota(jnp.int32, (1, 8 * DB), 1)
+        low_order = held[g, 0:1, pl.ds(at, 8 * DB)]
+        low_order = jnp.where(low_order < z.orders // 2, low_order, 0)
+        half = (col // (2 * DB)) % 2
+        m = jnp.where(half == 0, low_order, z.orders - 1 - low_order).astype(jnp.float32)
+        phase = (((col // DB) % 2) * (z.lon // 4)).astype(jnp.float32)
 
         def one(s, _):
             top = pl.multiple_of(s * tall, 16)
@@ -125,11 +137,12 @@
     def transform(g):
         def chunk(c, _):
             n = g * z.chunks + c
-            slot = lax.rem(n, 2)
-
-            @pl.when(n + 1 < total_steps)
-            def _():
-                field_copy(n + 1, lax.rem(n + 1, 2)).start()
+            slot = lax.rem(n, SLOTS)
+            ahead = n + SLOTS - 1
+
+            @pl.when(ahead < total_steps)
+            def _():
+                field_copy(ahead, lax.rem(ahead, SLOTS)).start()
 
             @pl.when(c == 0)
             def _():
@@ -185,7 +198,7 @@
 
     def ship(g):
         slot = lax.rem(g, 2)
-        for piece, (at, size) in enumerate(z.pieces):
+        for piece, at, size in z.sends:
 
             def issue(n, _):
                 d = partner(n)
@@ -225,8 +238,10 @@
     def left_factor(g, b):
         build_select(b)
         leg_copy(g, b).wait()
-        first = bounds[0, g * PER + b]
-        second = bounds[1, g * PER + b]
+        p = order[me * z.own + g * PER + b]
+        live = p < z.orders // 2
+        first = jnp.where(live, z.orders - p, 0)
+        second = jnp.where(live, z.orders - p, 4 * z.deg)
         in_first = marks[b, 1:2, :] == 0
         for lo, hi in spans:
             spread = jnp.dot(pbuf[lo:hi, :], sel[...], preferred_element_type=jnp.float32)
@@ -297,21 +312,9 @@
     z = Sizes(
         field.shape, legendre.shape, lax.axis_size("lat"), lax.axis_size("ch")
     )
-    me = lax.axis_index("lat") * z.nc + lax.axis_index("ch")
-    keep = pair_order < z.orders // 2
-    first = jnp.where(keep, pair_order, 0)
-    both = jnp.stack([first, z.orders - 1 - first], axis=1)
-    cols = both.reshape(z.blocks, DB, z.groups, PER, 2).transpose(2, 0, 3, 4, 1)
-    cols = jnp.broadcast_to(cols[:, :, :, :, None, :], cols.shape[:4] + (2, DB))
-    cols = cols.reshape(z.groups, z.blocks * 8 * DB).astype(jnp.float32)
-    turn = np.arange(z.blocks * 8 * DB) // DB % 2 * (z.lon // 4)
-    turn = jnp.broadcast_to(jnp.asarray(turn, jnp.float32), cols.shape)
-    mrow = jnp.stack([cols, turn], axis=1)
-    far = 4 * z.deg
-    lims = jnp.stack(
-        [jnp.where(keep, z.orders - first, 0), jnp.where(keep, z.orders - first, far)]
-    )
-    bounds = lax.dynamic_slice_in_dim(lims, me * z.own, z.own, axis=1)
+    held = pair_order.reshape(z.blocks, DB, z.groups, PER).transpose(2, 0, 3, 1)
+    held = jnp.broadcast_to(held[:, :, :, None, :], (z.groups, z.blocks, PER, 4, DB))
+    held = held.reshape(z.groups, 1, z.blocks * 8 * DB)
 
     col = np.arange(z.depth)
     marks = np.zeros((PER, 8, z.depth), np.int32)
@@ -332,7 +335,7 @@
         in_specs=[hbm, hbm, vmem, vmem, pl.BlockSpec(memory_space=pltpu.SMEM)],
         out_specs=vmem,
         scratch_shapes=[
-            pltpu.VMEM((2, z.cpad, z.lon), bf),
+            pltpu.VMEM((SLOTS, z.cpad, z.lon), bf),
             pltpu.VMEM((z.blocks, z.lon, 8 * DB), bf),
             pltpu.VMEM((z.nd * z.zrows, LANES), f32),
             pltpu.VMEM((2, z.nd, z.zrows, LANES), bf),
@@ -340,13 +343,13 @@
             pltpu.VMEM((z.latp, z.depth), bf),
             pltpu.VMEM((z.deg, z.latp), bf),
             pltpu.VMEM((PER, z.deg, z.depth), bf),
-            dma((2,)), dma, dma((2,)), dma((z.groups, len(z.pieces))),
+            dma((SLOTS,)), dma, dma((2,)), dma((z.groups, len(z.pieces))),
         ],
         compiler_params=pltpu.CompilerParams(
-            collective_id=0, has_side_effects=True, vmem_limit_bytes=67043328 - 4 * LANES * z.groups * z.orows - (1 << 19)
+            collective_id=0, has_side_effects=True, vmem_limit_bytes=67043328 - 4 * LANES * z.groups * z.orows - (1 << 18)
         ),
     )(
-        field.reshape(z.rows * z.chan, z.lon), legendre, mrow, jnp.asarray(marks), bounds
+        field.reshape(z.rows * z.chan, z.lon), legendre, held, jnp.asarray(marks), pair_order
     )
     shaped = flat.reshape(z.own, z.deg, z.ct, 2, LANES).transpose(0, 1, 3, 2, 4)
     return shaped.reshape(z.own, z.deg, 2, z.ct * LANES)

time: 427 us -> 418 us (0.979)
  Pallas kernels: 415 us -> 409 us
    pallas_call x1, Pallas kernels: 415 us -> 409 us  [per_device(): pl.pallas_call(functools.partial(kernel, z), out_shape=pltpu.VMEM((z.grou...]
where the time goes in v3:
time: 418 us
  Pallas kernels  409 us (98%)
  local copies, waits for them, and re-layouts  8.1 us (2%)
    pallas_call x1, Pallas kernels, per_device(): pl.pallas_call(functools.partial(kernel, z), out_shape=pltpu.VMEM((z.grou...  409 us

profile of v3, /device:TPU:0, one launch (start us, length us, event | category | flops | bytes accessed | tf_op | source)
XLA Modules:
  0.0 417.6 jit_solution(16963194048031230230)
XLA Ops:
  0.0 0.8 reshape.20
  0.8 0.1 copy.6
  0.9 0.7 broadcast_in_dim.12.held
  1.6 409.5 %shard_map.46 = f32[34608,128]{1,0:T(8,128)S(1)} custom-call(bf16[5824,1440]{1,0:T(8,128)(2,1)} %bitcast.10, bf16[12,721,728]{2,1,0:T(8,128)(2,1)} %leg.1, s32[6,1,256]{2,1,0:T(1,128)} %broadcast_in_dim.12.held, s32[2,8,1536]{2,1,0:T(8,128)} %constant.2.clone.marks, s32[384]{0:T(512)} %order.1), custom_call_target="tpu_custom_call" | custom-call | tf_op jit(solution)/shard_map/pallas_call | solution.py:332
  411.1 6.5 %copy.9 = f32[12,721,2,256]{3,2,1,0:T(2,128)} copy(f32[12,721,2,256]{3,2,1,0:T(2,128)S(1)} %bitcast.9) | data formatting | bytes 35438592
  (1 shorter events, 0.0 us)
